TPU v7x, 32 devices: a whole 2x2x4 slice. The times are simulated.
32 devices in a mesh: row: 4 (over z), col: 8 (over y, x, core).
Axes of the slice: x: 2, y: 2, z: 4, core: 2. Of those that a mesh axis runs over, the one named last changes fastest.
Arguments:
- node_latent: bfloat16 [32768, 128], P(('row', 'col')), may hold values from -6 to 6
- edge_latent: bfloat16 [131072, 128], P(('row', 'col')), may hold values from -6 to 6
- senders: int32 [131072], P(('row', 'col')), may hold values from 0 to 1535
- receivers: int32 [131072], P(('row', 'col')), may hold values from 0 to 1023
- send_index: int32 [32, 4, 128], P(('row', 'col')), may hold values from 0 to 1023
- context_table: bfloat16 [256, 128], P(('row', 'col')), may hold values from -6 to 6
- region: int32 [32768], P(('row', 'col')), may hold values from 0 to 255
- edge_w1: bfloat16 [2, 384, 128], replicated, may hold values from -0.3125 to 0.3125
- edge_w2: bfloat16 [2, 128, 128], replicated, may hold values from -0.5 to 0.5
- edge_bias: float32 [2, 3, 128], replicated, may hold values from -3 to 3
- edge_gain: float32 [2, 128], replicated, may hold values from 0.25 to 1.75
- node_w1: bfloat16 [2, 384, 128], replicated, may hold values from -0.3125 to 0.3125
- node_wg: bfloat16 [2, 128, 128], replicated, may hold values from -0.5 to 0.5
- node_w2: bfloat16 [2, 128, 128], replicated, may hold values from -0.5 to 0.5
- node_bias: float32 [2, 3, 128], replicated, may hold values from -3 to 3
- node_gain: float32 [2, 128], replicated, may hold values from 0.25 to 1.75
Outputs:
- node_out: bfloat16 [32768, 128], P(('row', 'col'))
- edge_out: bfloat16 [131072, 128], P(('row', 'col'))
Inputs may be any that keep to these rules, and one draw needn't show every extreme that they name: senders index the extended table of the edge's own partition: below 1024 its own nodes, then the four received blocks of 128 rows in the order above, below, left, right. receivers are nodes of the edge's own partition. `send_index`: rows of the sending partition's own nodes; repeats may occur.
All inputs are finite; a program needn't handle non-finite values.
Results may differ from a plain program's by a relative error of at most 0.0085.
Values may be sent and summed in bfloat16 or wider, within the bound.
A program may use at most 64 MiB of HBM per device.

v0:
```python
import math
import jax
import jax.numpy as jnp
from jax import lax
from jax.sharding import PartitionSpec as P

LAYERS = 2
EPS = 1e-05


def passed_along(value, axis, by):
    devices = lax.axis_size(axis)
    pairs = [(i, i + by) for i in range(devices) if 0 <= i + by < devices]
    return lax.ppermute(value, axis, pairs)


def norm_tail(pre, w_out, b_out, gain, shift):
    hidden = jax.nn.relu(pre).astype(jnp.bfloat16)
    y_val = jnp.dot(hidden, w_out, preferred_element_type=jnp.float32) + b_out
    centred = y_val - jnp.mean(y_val, axis=-1, keepdims=True)
    spread = jnp.mean(centred * centred, axis=-1, keepdims=True)
    return centred * lax.rsqrt(spread + EPS) * gain + shift


def one_hot(index, count):
    columns = lax.broadcasted_iota(jnp.int32, (1, count), 1)
    return (index[:, None] == columns).astype(jnp.bfloat16)


def lookup(index, table):
    picker = one_hot(index, table.shape[0])
    return jnp.dot(picker, table, preferred_element_type=jnp.float32).astype(jnp.bfloat16)


def blocked_lookup(index, table):
    total_rows = index.shape[0]
    block_rows = math.gcd(total_rows, 512)
    pieces = index.reshape(total_rows // block_rows, block_rows)
    result = lax.map(lambda piece: lookup(piece, table), pieces)
    return result.reshape(total_rows, table.shape[1])


def edge_and_sum(extended, nodes, edges, senders, receivers, w_in, w_out, bias, gain):
    total_rows = edges.shape[0]
    width = edges.shape[1]
    node_count = nodes.shape[0]
    block_rows = math.gcd(total_rows, 512)
    blocks = total_rows // block_rows

    def one_block(summed, items):
        edge_rows, send_rows, recv_rows = items
        recv_hot = one_hot(recv_rows, node_count)
        sender_feats = lookup(send_rows, extended)
        receiver_feats = jnp.dot(recv_hot, nodes, preferred_element_type=jnp.float32).astype(
            jnp.bfloat16
        )
        feats = jnp.concatenate([sender_feats, receiver_feats, edge_rows], axis=1)
        pre = jnp.dot(feats, w_in, preferred_element_type=jnp.float32) + bias[0]
        fresh = (
            edge_rows.astype(jnp.float32) + norm_tail(pre, w_out, bias[1], gain, bias[2])
        ).astype(jnp.bfloat16)
        added = lax.dot_general(
            recv_hot, fresh, (((0,), (0,)), ((), ())), preferred_element_type=jnp.float32
        )
        return (summed + added, fresh)

    start = jnp.zeros((node_count, width), jnp.float32)
    items = (
        edges.reshape(blocks, block_rows, width),
        senders.reshape(blocks, block_rows),
        receivers.reshape(blocks, block_rows),
    )
    summed, fresh = lax.scan(one_block, start, items)
    return (fresh.reshape(total_rows, width), summed.astype(jnp.bfloat16))


def node_step(nodes, summed, context_rows, w_in, w_out, bias, gain, shift_in):
    feats = jnp.concatenate([nodes, summed, context_rows], axis=1)
    pre = jnp.dot(feats, w_in, preferred_element_type=jnp.float32) + shift_in
    return (nodes.astype(jnp.float32) + norm_tail(pre, w_out, bias[1], gain, bias[2])).astype(
        jnp.bfloat16
    )


def row_move(block, offset):
    return passed_along(block, "row", offset)


def col_move(block, offset):
    return passed_along(block, "col", offset)


def extend(nodes, send_index):
    count = send_index.shape[2]
    width = nodes.shape[1]
    picked = lookup(send_index.reshape(-1), nodes).reshape(4, count, width)
    return jnp.concatenate(
        [
            nodes,
            row_move(picked[0], 1),
            row_move(picked[1], -1),
            col_move(picked[2], 1),
            col_move(picked[3], -1),
        ],
        axis=0,
    )


def local(
    node_latent,
    edge_latent,
    senders,
    receivers,
    send_index,
    context_table,
    region,
    edge_w1,
    edge_w2,
    edge_bias,
    edge_gain,
    node_w1,
    node_wg,
    node_w2,
    node_bias,
    node_gain,
):
    width = node_latent.shape[1]
    local_sum = jnp.sum(node_latent.astype(jnp.float32), axis=0)
    total = lax.psum(local_sum, ("row", "col"))
    by_row = lax.all_gather(context_table[None], "row", axis=0, tiled=True)
    table = lax.all_gather(by_row, "col", axis=1, tiled=True).reshape(-1, width)
    node_count = node_latent.shape[0] * lax.axis_size("row") * lax.axis_size("col")
    pooled = total / math.sqrt(node_count)
    context_rows = blocked_lookup(region, table)
    nodes = node_latent
    edges = edge_latent
    for layer in range(LAYERS):
        extended = extend(nodes, send_index)
        edges, summed = edge_and_sum(
            extended,
            nodes,
            edges,
            senders,
            receivers,
            edge_w1[layer],
            edge_w2[layer],
            edge_bias[layer],
            edge_gain[layer],
        )
        shift_in = node_bias[layer, 0] + jnp.dot(
            pooled, node_wg[layer].astype(jnp.float32), precision=lax.Precision.HIGHEST
        )
        nodes = node_step(
            nodes,
            summed,
            context_rows,
            node_w1[layer],
            node_w2[layer],
            node_bias[layer],
            node_gain[layer],
            shift_in,
        )
    return (nodes, edges)


def solution(mesh):
    return jax.shard_map(
        local,
        mesh=mesh,
        in_specs=(
            P(("row", "col"), None),
            P(("row", "col"), None),
            P(("row", "col")),
            P(("row", "col")),
            P(("row", "col"), None, None),
            P(("row", "col"), None),
            P(("row", "col")),
            P(),
            P(),
            P(),
            P(),
            P(),
            P(),
            P(),
            P(),
            P(),
        ),
        out_specs=(P(("row", "col"), None), P(("row", "col"), None)),
        check_vma=False,
    )
```

profile of v0, /device:TPU:11, one launch (start us, length us, event | category | flops | bytes accessed | tf_op | source)
XLA Modules:
  0.0 200.9 jit_solution(13532602859649688257)
XLA Ops:
  0.7 1.5 fusion.61
  2.9 3.2 %collective-permute-start = (bf16[128,128]{1,0:T(8,128)(2,1)}, bf16[128,128]{1,0:T(8,128)(2,1)S(1)}, u32[]{:S(2)}, u32[]{:S(2)}) collective-permute-start(bf16[128,128]{1,0:T(8,128)(2,1)} %get-tuple-element.356), channel_id=1, source_target_pairs={{0,8},{8,16},{16,24},{1,9},{9,17},{17,25},{2,10},{10,18},{18,26},{... | collective-permute-start | bytes 98312 | tf_op jit(solution)/shard_map/ppermute | solution.py:14
  6.1 2.1 %collective-permute-start.1 = (bf16[128,128]{1,0:T(8,128)(2,1)}, bf16[128,128]{1,0:T(8,128)(2,1)S(1)}, u32[]{:S(2)}, u32[]{:S(2)}) collective-permute-start(bf16[128,128]{1,0:T(8,128)(2,1)} %get-tuple-element.355), channel_id=1, source_target_pairs={{8,0},{16,8},{24,16},{9,1},{17,9},{25,17},{10,2},{18,10},{26,18},{... | collective-permute-start | bytes 98312 | tf_op jit(solution)/shard_map/ppermute | solution.py:14
  8.2 4.2 %collective-permute-start.2 = (bf16[128,128]{1,0:T(8,128)(2,1)S(1)}, bf16[128,128]{1,0:T(8,128)(2,1)S(1)}, u32[]{:S(2)}, u32[]{:S(2)}) collective-permute-start(bf16[128,128]{1,0:T(8,128)(2,1)S(1)} %get-tuple-element.354), channel_id=1, source_target_pairs={{0,1},{1,2},{2,3},{3,4},{4,5},{5,6},{6,7},{8,9},{9,10},{10,11},{11... | collective-permute-start | bytes 98312 | tf_op jit(solution)/shard_map/ppermute | solution.py:14
  12.4 1.9 collective-permute-start.3
  15.4 40.4 %psum.7 = f32[128]{0:T(128)S(1)} all-reduce(f32[128]{0:T(128)S(1)} %convert_reduce_fusion), channel_id=1, replica_groups=mesh['row'=4,'col'=8] {'row','col'}, use_global_device_ids=true, to_apply=%region_7.8 | all-reduce | flops 128 | bytes 1024 | tf_op jit(solution)/shard_map/psum | solution.py:129
  56.3 8.2 %all-gather = bf16[32,128]{1,0:T(8,128)(2,1)S(1)} all-gather(bf16[8,128]{1,0:T(8,128)(2,1)S(1)} %copy-done.10), channel_id=2, replica_groups=mesh['row'=4,'col'=8] {'row'}, dimensions={0}, use_global_device_ids=true | all-gather | bytes 10240 | tf_op jit(solution)/shard_map/all_gather | solution.py:130
  64.5 12.8 %all_gather.7 = bf16[4,64,128]{2,1,0:T(8,128)(2,1)S(1)} all-gather(bf16[4,8,128]{2,1,0:T(8,128)(2,1)S(1)} %bitcast.189), channel_id=1, replica_groups=mesh['row'=4,'col'=8] {'col'}, dimensions={1}, use_global_device_ids=true | all-gather | bytes 73728 | tf_op jit(solution)/shard_map/all_gather | solution.py:131
  79.1 50.7 %while.37 = (s32[]{:T(128)}, f32[1024,128]{1,0:T(8,128)S(1)}, bf16[8,512,128]{1,2,0:T(8,128)(2,1)S(1)}, s32[8,512]{1,0:T(8,128)S(1)}, bf16[8,512,128]{2,1,0:T(8,...) while((s32[]{:T(128)}, f32[1024,128]{1,0:T(8,128)S(1)}, ...), condition=%wide.region_3.4_spmd.clone, body=%wide.region_0.3_spmd.clone.sunk | while | flops 541786624 | bytes 4363419 | solution.py:73
  80.4 1.5 fusion.176
  82.9 1.4 fusion.177
  86.7 1.5 fusion.176
  89.3 1.4 fusion.177
  93.1 1.5 fusion.176
  95.6 1.4 fusion.177
  99.4 1.5 fusion.176
  101.9 1.4 fusion.177
  105.7 1.5 fusion.176
  108.3 1.4 fusion.177
  112.0 1.5 fusion.176
  114.6 1.4 fusion.177
  118.4 1.5 fusion.176
  120.9 1.4 fusion.177
  124.7 1.5 fusion.176
  127.3 1.4 fusion.177
  129.9 1.5 fusion.125
  132.8 2.8 %collective-permute-start.4 = (bf16[128,128]{0,1:T(8,128)(2,1)S(1)}, bf16[128,128]{0,1:T(8,128)(2,1)S(1)}, u32[]{:S(2)}, u32[]{:S(2)}) collective-permute-start(bf16[128,128]{0,1:T(8,128)(2,1)S(1)} %get-tuple-element.352), channel_id=1, source_target_pairs={{0,8},{8,16},{16,24},{1,9},{9,17},{17,25},{2,10},{10,18},{18,26},{... | collective-permute-start | bytes 98312 | tf_op jit(solution)/shard_map/ppermute | solution.py:14
  136.5 2.5 %collective-permute-start.5 = (bf16[128,128]{0,1:T(8,128)(2,1)S(1)}, bf16[128,128]{0,1:T(8,128)(2,1)S(1)}, u32[]{:S(2)}, u32[]{:S(2)}) collective-permute-start(bf16[128,128]{0,1:T(8,128)(2,1)S(1)} %get-tuple-element.351), channel_id=1, source_target_pairs={{8,0},{16,8},{24,16},{9,1},{17,9},{25,17},{10,2},{18,10},{26,18},{... | collective-permute-start | bytes 98312 | tf_op jit(solution)/shard_map/ppermute | solution.py:14
  139.1 3.7 %collective-permute-start.6 = (bf16[128,128]{0,1:T(8,128)(2,1)S(1)}, bf16[128,128]{0,1:T(8,128)(2,1)S(1)}, u32[]{:S(2)}, u32[]{:S(2)}) collective-permute-start(bf16[128,128]{0,1:T(8,128)(2,1)S(1)} %get-tuple-element.350), channel_id=1, source_target_pairs={{0,1},{1,2},{2,3},{3,4},{4,5},{5,6},{6,7},{8,9},{9,10},{10,11},{11... | collective-permute-start | bytes 98312 | tf_op jit(solution)/shard_map/ppermute | solution.py:14
  142.8 1.9 collective-permute-start.7
  144.8 4.1 %collective-permute-done.7 = bf16[128,128]{0,1:T(8,128)(2,1)S(1)} collective-permute-done((bf16[128,128]{0,1:T(8,128)(2,1)S(1)}, bf16[128,128]{0,1:T(8,128)(2,1)S(1)}, u32[]{:S(2)}, u32[]{:S(2)}) %collective-permute-start.7) | collective-permute-done | bytes 32800 | tf_op jit(solution)/shard_map/ppermute | solution.py:14
  149.2 49.0 %while.38 = (s32[]{:T(128)}, f32[1024,128]{1,0:T(8,128)S(1)}, bf16[8,512,128]{2,1,0:T(8,128)(2,1)}, s32[8,512]{1,0:T(8,128)S(1)}, bf16[8,512,128]{1,2,0:T(8,128)...) while((s32[]{:T(128)}, f32[1024,128]{1,0:T(8,128)S(1)}, ...), condition=%wide.region_13.14_spmd.clone, body=%wide.region_10.13_spmd.clone.sunk | while | flops 541786624 | bytes 4495003 | solution.py:73
  150.5 1.5 fusion.186
  152.0 1.5 fusion.187
  156.6 1.5 fusion.186
  158.2 1.5 fusion.187
  162.7 1.5 fusion.186
  164.3 1.5 fusion.187
  168.8 1.5 fusion.186
  170.4 1.5 fusion.187
  175.0 1.5 fusion.186
  176.5 1.5 fusion.187
  181.1 1.5 fusion.186
  182.6 1.5 fusion.187
  187.2 1.5 fusion.186
  188.8 1.5 fusion.187
  193.3 1.5 fusion.186
  194.9 1.5 fusion.187
  (265 shorter events, 60.7 us)
Async XLA Ops:
  0.6 13.7 %copy-start = (bf16[1024,128]{1,0:T(8,128)(2,1)S(1)}, bf16[1024,128]{1,0:T(8,128)(2,1)}, u32[]{:S(2)}) copy-start(bf16[1024,128]{1,0:T(8,128)(2,1)} %param.22) | copy-start | bytes 786436
  0.6 13.9 %copy-start.1 = (bf16[2,384,128]{2,1,0:T(8,128)(2,1)S(1)}, bf16[2,384,128]{2,1,0:T(8,128)(2,1)}, u32[]{:S(2)}) copy-start(bf16[2,384,128]{2,1,0:T(8,128)(2,1)} %param.29) | copy-start | bytes 589828
  0.7 13.9 %copy-start.2 = (bf16[2,128,128]{2,1,0:T(8,128)(2,1)S(1)}, bf16[2,128,128]{2,1,0:T(8,128)(2,1)}, u32[]{:S(2)}) copy-start(bf16[2,128,128]{2,1,0:T(8,128)(2,1)} %param.30) | copy-start | bytes 196612
  0.7 14.5 %copy-start.7 = (f32[2,3,128]{2,0,1:T(2,128)S(1)}, f32[2,3,128]{2,0,1:T(2,128)}, u32[]{:S(2)}) copy-start(f32[2,3,128]{2,0,1:T(2,128)} %param.31) | copy-start | bytes 9220
  0.7 14.5 %copy-start.12 = (f32[2,128]{1,0:T(2,128)S(1)}, f32[2,128]{1,0:T(2,128)}, u32[]{:S(2)}) copy-start(f32[2,128]{1,0:T(2,128)} %param.32) | copy-start | bytes 3076
  2.2 53.5 %copy-start.11 = (f32[2,3,128]{2,0,1:T(2,128)S(1)}, f32[2,3,128]{2,0,1:T(2,128)}, u32[]{:S(2)}) copy-start(f32[2,3,128]{2,0,1:T(2,128)} %param.36) | copy-start | bytes 9220
  2.2 54.1 %copy-start.10 = (bf16[8,128]{1,0:T(8,128)(2,1)S(1)}, bf16[8,128]{1,0:T(8,128)(2,1)}, u32[]{:S(2)}) copy-start(bf16[8,128]{1,0:T(8,128)(2,1)} %param.27) | copy-start | bytes 6148
  2.2 75.0 %copy-start.6 = (s32[1024]{0:T(1024)S(1)}, s32[1024]{0:T(1024)}, u32[]{:S(2)}) copy-start(s32[1024]{0:T(1024)} %param.28) | copy-start | bytes 12292
  2.9 76.1 %collective-permute-start = (bf16[128,128]{1,0:T(8,128)(2,1)}, bf16[128,128]{1,0:T(8,128)(2,1)S(1)}, u32[]{:S(2)}, u32[]{:S(2)}) collective-permute-start(bf16[128,128]{1,0:T(8,128)(2,1)} %get-tuple-element.356), channel_id=1, source_target_pairs={{0,8},{8,16},{16,24},{1,9},{9,17},{17,25},{2,10},{10,18},{18,26},{... | collective-permute-start | bytes 98312 | tf_op jit(solution)/shard_map/ppermute | solution.py:14
  6.1 72.9 %collective-permute-start.1 = (bf16[128,128]{1,0:T(8,128)(2,1)}, bf16[128,128]{1,0:T(8,128)(2,1)S(1)}, u32[]{:S(2)}, u32[]{:S(2)}) collective-permute-start(bf16[128,128]{1,0:T(8,128)(2,1)} %get-tuple-element.355), channel_id=1, source_target_pairs={{8,0},{16,8},{24,16},{9,1},{17,9},{25,17},{10,2},{18,10},{26,18},{... | collective-permute-start | bytes 98312 | tf_op jit(solution)/shard_map/ppermute | solution.py:14
  8.2 70.8 %collective-permute-start.2 = (bf16[128,128]{1,0:T(8,128)(2,1)S(1)}, bf16[128,128]{1,0:T(8,128)(2,1)S(1)}, u32[]{:S(2)}, u32[]{:S(2)}) collective-permute-start(bf16[128,128]{1,0:T(8,128)(2,1)S(1)} %get-tuple-element.354), channel_id=1, source_target_pairs={{0,1},{1,2},{2,3},{3,4},{4,5},{5,6},{6,7},{8,9},{9,10},{10,11},{11... | collective-permute-start | bytes 98312 | tf_op jit(solution)/shard_map/ppermute | solution.py:14
  12.4 66.6 %collective-permute-start.3 = (bf16[128,128]{1,0:T(8,128)(2,1)S(1)}, bf16[128,128]{1,0:T(8,128)(2,1)S(1)}, u32[]{:S(2)}, u32[]{:S(2)}) collective-permute-start(bf16[128,128]{1,0:T(8,128)(2,1)S(1)} %get-tuple-element.353), channel_id=1, source_target_pairs={{1,0},{2,1},{3,2},{4,3},{5,4},{6,5},{7,6},{9,8},{10,9},{11,10},{12... | collective-permute-start | bytes 98312 | tf_op jit(solution)/shard_map/ppermute | solution.py:14
  15.2 62.7 %copy-start.13 = (f32[2,128]{1,0:T(2,128)S(1)}, f32[2,128]{1,0:T(2,128)}, u32[]{:S(2)}) copy-start(f32[2,128]{1,0:T(2,128)} %param.37) | copy-start | bytes 3076
  15.2 63.3 %copy-start.16 = (bf16[2,128,128]{2,1,0:T(8,128)(2,1)S(1)}, bf16[2,128,128]{2,1,0:T(8,128)(2,1)}, u32[]{:S(2)}) copy-start(bf16[2,128,128]{2,1,0:T(8,128)(2,1)} %param.34) | copy-start | bytes 196612
  77.3 1.5 copy-start.4
  77.3 1.5 copy-start.5
  129.9 1.7 copy-start.8
  129.9 1.7 copy-start.9
  131.4 0.7 copy-start.18
  131.5 4.0 %copy-start.17 = (bf16[2,128,128]{2,1,0:T(8,128)(2,1)S(1)}, bf16[2,128,128]{2,1,0:T(8,128)(2,1)}, u32[]{:S(2)}) copy-start(bf16[2,128,128]{2,1,0:T(8,128)(2,1)} %param.34) | copy-start | bytes 196612
  132.7 16.4 %copy-start.3 = (bf16[128,128]{1,0:T(8,128)(2,1)S(1)}, bf16[128,128]{1,0:T(8,128)(2,1)}, u32[]{:S(2)}) copy-start(bf16[128,128]{1,0:T(8,128)(2,1)} %get-tuple-element.643) | copy-start | bytes 98308
  132.8 11.9 %collective-permute-start.4 = (bf16[128,128]{0,1:T(8,128)(2,1)S(1)}, bf16[128,128]{0,1:T(8,128)(2,1)S(1)}, u32[]{:S(2)}, u32[]{:S(2)}) collective-permute-start(bf16[128,128]{0,1:T(8,128)(2,1)S(1)} %get-tuple-element.352), channel_id=1, source_target_pairs={{0,8},{8,16},{16,24},{1,9},{9,17},{17,25},{2,10},{10,18},{18,26},{... | collective-permute-start | bytes 98312 | tf_op jit(solution)/shard_map/ppermute | solution.py:14
  136.5 8.2 %collective-permute-start.5 = (bf16[128,128]{0,1:T(8,128)(2,1)S(1)}, bf16[128,128]{0,1:T(8,128)(2,1)S(1)}, u32[]{:S(2)}, u32[]{:S(2)}) collective-permute-start(bf16[128,128]{0,1:T(8,128)(2,1)S(1)} %get-tuple-element.351), channel_id=1, source_target_pairs={{8,0},{16,8},{24,16},{9,1},{17,9},{25,17},{10,2},{18,10},{26,18},{... | collective-permute-start | bytes 98312 | tf_op jit(solution)/shard_map/ppermute | solution.py:14
  139.1 5.7 %collective-permute-start.6 = (bf16[128,128]{0,1:T(8,128)(2,1)S(1)}, bf16[128,128]{0,1:T(8,128)(2,1)S(1)}, u32[]{:S(2)}, u32[]{:S(2)}) collective-permute-start(bf16[128,128]{0,1:T(8,128)(2,1)S(1)} %get-tuple-element.350), channel_id=1, source_target_pairs={{0,1},{1,2},{2,3},{3,4},{4,5},{5,6},{6,7},{8,9},{9,10},{10,11},{11... | collective-permute-start | bytes 98312 | tf_op jit(solution)/shard_map/ppermute | solution.py:14
  142.8 6.1 %collective-permute-start.7 = (bf16[128,128]{0,1:T(8,128)(2,1)S(1)}, bf16[128,128]{0,1:T(8,128)(2,1)S(1)}, u32[]{:S(2)}, u32[]{:S(2)}) collective-permute-start(bf16[128,128]{0,1:T(8,128)(2,1)S(1)} %get-tuple-element.349), channel_id=1, source_target_pairs={{1,0},{2,1},{3,2},{4,3},{5,4},{6,5},{7,6},{9,8},{10,9},{11,10},{12... | collective-permute-start | bytes 98312 | tf_op jit(solution)/shard_map/ppermute | solution.py:14
  149.1 49.1 %copy-start.14 = (f32[128]{0:T(128)S(1)}, f32[128]{0:T(128)}, u32[]{:S(2)}) copy-start(f32[128]{0:T(128)} %get-tuple-element.362) | copy-start | bytes 1540
  149.2 49.1 %copy-start.15 = (bf16[2,384,128]{2,1,0:T(8,128)(2,1)S(1)}, bf16[2,384,128]{2,1,0:T(8,128)(2,1)}, u32[]{:S(2)}) copy-start(bf16[2,384,128]{2,1,0:T(8,128)(2,1)} %param.33) | copy-start | bytes 589828
where the time goes:
time: 202 us; the launch traced here: 201 us
  matrix products  87.2 us (43%)
  blocking collectives  61.3 us (30%)
  starting transfers between devices  22.3 us (11%)
  local copies, waits for them, and re-layouts  19.7 us (10%)
  waiting for transfers between devices  4.14 us (2%)
  other arithmetic  3.71 us (2%)
    psum x1, blocking collectives, local(): total = lax.psum(local_sum, ('row', 'col'))  40.4 us
    dot_general x20, matrix products, lookup(): jnp.dot(picker, table, preferred_element_type=jnp.float32)  27 us
    dot_general x18, matrix products, norm_tail(): y_val = jnp.dot(hidden, w_out, preferred_element_type=jnp.float32) + b_out  26.1 us
    ppermute x8, starting transfers between devices, passed_along(): return lax.ppermute(value, axis, pairs)  22.3 us
    dot_general x16, matrix products, one_block(): jnp.dot(recv_hot, nodes, preferred_element_type=jnp.float32)  20.8 us
    all_gather x1, blocking collectives, local(): table = lax.all_gather(by_row, 'col', axis=1, tiled=True).reshape(-1, width)  12.8 us
    dot_general x16, matrix products, one_block(): lax.dot_general(recv_hot, fresh, (((0,), (0,)), ((), ())), preferred_elem...  12.3 us
    dynamic_slice x32, local copies, waits for them, and re-layouts, edge_and_sum(): summed, fresh = lax.scan(one_block, start, items)  8.37 us
  transfers between devices with their start and end apart: 8, of which 1 were waited for; matrix products, arithmetic and copies ran while one was open for 2% of the time, Pallas kernels for 0%

commit v1 on v0

--- a/solution.py
+++ b/solution.py
@@ -126,7 +126,7 @@
 ):
     width = node_latent.shape[1]
     local_sum = jnp.sum(node_latent.astype(jnp.float32), axis=0)
-    total = lax.psum(local_sum, ("row", "col"))
+    total = lax.psum(lax.psum(local_sum, "row"), "col")
     by_row = lax.all_gather(context_table[None], "row", axis=0, tiled=True)
     table = lax.all_gather(by_row, "col", axis=1, tiled=True).reshape(-1, width)
     node_count = node_latent.shape[0] * lax.axis_size("row") * lax.axis_size("col")

time: 202 us -> 183 us (0.906)
  blocking collectives: 61.3 us -> 42.2 us
    psum x1 -> x2, blocking collectives: 40.4 us -> 20.3 us  [local(): total = lax.psum(lax.psum(local_sum, 'row'), 'col')]
where the time goes in v1:
time: 183 us; the launch traced here: 182 us
  matrix products  87 us (48%)
  blocking collectives  42.2 us (23%)
  starting transfers between devices  22.6 us (12%)
  local copies, waits for them, and re-layouts  19.7 us (11%)
  waiting for transfers between devices  4.14 us (2%)
  other arithmetic  3.71 us (2%)
    dot_general x20, matrix products, lookup(): jnp.dot(picker, table, preferred_element_type=jnp.float32)  26.9 us
    dot_general x18, matrix products, norm_tail(): y_val = jnp.dot(hidden, w_out, preferred_element_type=jnp.float32) + b_out  26.1 us
    ppermute x8, starting transfers between devices, passed_along(): return lax.ppermute(value, axis, pairs)  22.6 us
    dot_general x16, matrix products, one_block(): jnp.dot(recv_hot, nodes, preferred_element_type=jnp.float32)  20.7 us
    psum x2, blocking collectives, local(): total = lax.psum(lax.psum(local_sum, 'row'), 'col')  20.3 us
    dot_general x16, matrix products, one_block(): lax.dot_general(recv_hot, fresh, (((0,), (0,)), ((), ())), preferred_elem...  12.3 us
    all_gather x1, blocking collectives, local(): table = lax.all_gather(by_row, 'col', axis=1, tiled=True).reshape(-1, width)  12 us
    all_gather x1, blocking collectives, local(): by_row = lax.all_gather(context_table[None], 'row', axis=0, tiled=True)  9.91 us
  transfers between devices with their start and end apart: 8, of which 1 were waited for; matrix products, arithmetic and copies ran while one was open for 2% of the time, Pallas kernels for 0%

profile of v1, /device:TPU:11, one launch (start us, length us, event | category | flops | bytes accessed | tf_op | source)
XLA Modules:
  0.0 181.8 jit_solution(10107419600586527363)
XLA Ops:
  0.7 1.5 fusion.61
  2.9 3.2 %collective-permute-start = (bf16[128,128]{1,0:T(8,128)(2,1)}, bf16[128,128]{1,0:T(8,128)(2,1)S(1)}, u32[]{:S(2)}, u32[]{:S(2)}) collective-permute-start(bf16[128,128]{1,0:T(8,128)(2,1)} %get-tuple-element.356), channel_id=1, source_target_pairs={{0,8},{8,16},{16,24},{1,9},{9,17},{17,25},{2,10},{10,18},{18,26},{... | collective-permute-start | bytes 98312 | tf_op jit(solution)/shard_map/ppermute | solution.py:14
  6.1 2.1 %collective-permute-start.1 = (bf16[128,128]{1,0:T(8,128)(2,1)}, bf16[128,128]{1,0:T(8,128)(2,1)S(1)}, u32[]{:S(2)}, u32[]{:S(2)}) collective-permute-start(bf16[128,128]{1,0:T(8,128)(2,1)} %get-tuple-element.355), channel_id=1, source_target_pairs={{8,0},{16,8},{24,16},{9,1},{17,9},{25,17},{10,2},{18,10},{26,18},{... | collective-permute-start | bytes 98312 | tf_op jit(solution)/shard_map/ppermute | solution.py:14
  8.2 4.2 %collective-permute-start.2 = (bf16[128,128]{1,0:T(8,128)(2,1)S(1)}, bf16[128,128]{1,0:T(8,128)(2,1)S(1)}, u32[]{:S(2)}, u32[]{:S(2)}) collective-permute-start(bf16[128,128]{1,0:T(8,128)(2,1)S(1)} %get-tuple-element.354), channel_id=1, source_target_pairs={{0,1},{1,2},{2,3},{3,4},{4,5},{5,6},{6,7},{8,9},{9,10},{10,11},{11... | collective-permute-start | bytes 98312 | tf_op jit(solution)/shard_map/ppermute | solution.py:14
  12.4 1.9 %collective-permute-start.3 = (bf16[128,128]{1,0:T(8,128)(2,1)S(1)}, bf16[128,128]{1,0:T(8,128)(2,1)S(1)}, u32[]{:S(2)}, u32[]{:S(2)}) collective-permute-start(bf16[128,128]{1,0:T(8,128)(2,1)S(1)} %get-tuple-element.353), channel_id=1, source_target_pairs={{1,0},{2,1},{3,2},{4,3},{5,4},{6,5},{7,6},{9,8},{10,9},{11,10},{12... | collective-permute-start | bytes 98312 | tf_op jit(solution)/shard_map/ppermute | solution.py:14
  15.3 7.2 %psum.14 = f32[128]{0:T(128)S(1)} all-reduce(f32[128]{0:T(128)S(1)} %convert_reduce_fusion), channel_id=1, replica_groups=mesh['row'=4,'col'=8] {'row'}, use_global_device_ids=true, to_apply=%region_7.8 | all-reduce | flops 128 | bytes 1024 | tf_op jit(solution)/shard_map/psum | solution.py:129
  22.5 13.1 %psum.15 = f32[128]{0:T(128)S(1)} all-reduce(f32[128]{0:T(128)S(1)} %psum.14), channel_id=1, replica_groups=mesh['row'=4,'col'=8] {'col'}, use_global_device_ids=true, to_apply=%region_8.9 | all-reduce | flops 128 | bytes 1024 | tf_op jit(solution)/shard_map/psum | solution.py:129
  36.2 9.9 %all-gather = bf16[32,128]{1,0:T(8,128)(2,1)S(1)} all-gather(bf16[8,128]{1,0:T(8,128)(2,1)S(1)} %copy-done.10), channel_id=2, replica_groups=mesh['row'=4,'col'=8] {'row'}, dimensions={0}, use_global_device_ids=true | all-gather | bytes 10240 | tf_op jit(solution)/shard_map/all_gather | solution.py:130
  46.2 12.0 %all_gather.7 = bf16[4,64,128]{2,1,0:T(8,128)(2,1)S(1)} all-gather(bf16[4,8,128]{2,1,0:T(8,128)(2,1)S(1)} %bitcast.189), channel_id=1, replica_groups=mesh['row'=4,'col'=8] {'col'}, dimensions={1}, use_global_device_ids=true | all-gather | bytes 73728 | tf_op jit(solution)/shard_map/all_gather | solution.py:131
  59.9 50.7 %while.37 = (s32[]{:T(128)}, f32[1024,128]{1,0:T(8,128)S(1)}, bf16[8,512,128]{1,2,0:T(8,128)(2,1)S(1)}, s32[8,512]{1,0:T(8,128)S(1)}, bf16[8,512,128]{2,1,0:T(8,...) while((s32[]{:T(128)}, f32[1024,128]{1,0:T(8,128)S(1)}, ...), condition=%wide.region_3.4_spmd.clone, body=%wide.region_0.3_spmd.clone.sunk | while | flops 541786624 | bytes 4363419 | solution.py:73
  61.2 1.5 fusion.176
  63.7 1.5 fusion.177
  67.5 1.5 fusion.176
  70.1 1.4 fusion.177
  73.8 1.5 fusion.176
  76.4 1.4 fusion.177
  80.2 1.5 fusion.176
  82.7 1.4 fusion.177
  86.5 1.5 fusion.176
  89.1 1.4 fusion.177
  92.8 1.5 fusion.176
  95.4 1.4 fusion.177
  99.2 1.5 fusion.176
  101.7 1.4 fusion.177
  105.5 1.5 fusion.176
  110.7 1.5 fusion.125
  113.6 4.0 %collective-permute-start.4 = (bf16[128,128]{0,1:T(8,128)(2,1)S(1)}, bf16[128,128]{0,1:T(8,128)(2,1)S(1)}, u32[]{:S(2)}, u32[]{:S(2)}) collective-permute-start(bf16[128,128]{0,1:T(8,128)(2,1)S(1)} %get-tuple-element.352), channel_id=1, source_target_pairs={{0,8},{8,16},{16,24},{1,9},{9,17},{17,25},{2,10},{10,18},{18,26},{... | collective-permute-start | bytes 98312 | tf_op jit(solution)/shard_map/ppermute | solution.py:14
  118.5 1.9 %collective-permute-start.5 = (bf16[128,128]{0,1:T(8,128)(2,1)S(1)}, bf16[128,128]{0,1:T(8,128)(2,1)S(1)}, u32[]{:S(2)}, u32[]{:S(2)}) collective-permute-start(bf16[128,128]{0,1:T(8,128)(2,1)S(1)} %get-tuple-element.351), channel_id=1, source_target_pairs={{8,0},{16,8},{24,16},{9,1},{17,9},{25,17},{10,2},{18,10},{26,18},{... | collective-permute-start | bytes 98312 | tf_op jit(solution)/shard_map/ppermute | solution.py:14
  120.5 3.4 %collective-permute-start.6 = (bf16[128,128]{0,1:T(8,128)(2,1)S(1)}, bf16[128,128]{0,1:T(8,128)(2,1)S(1)}, u32[]{:S(2)}, u32[]{:S(2)}) collective-permute-start(bf16[128,128]{0,1:T(8,128)(2,1)S(1)} %get-tuple-element.350), channel_id=1, source_target_pairs={{0,1},{1,2},{2,3},{3,4},{4,5},{5,6},{6,7},{8,9},{9,10},{10,11},{11... | collective-permute-start | bytes 98312 | tf_op jit(solution)/shard_map/ppermute | solution.py:14
  123.9 1.9 %collective-permute-start.7 = (bf16[128,128]{0,1:T(8,128)(2,1)S(1)}, bf16[128,128]{0,1:T(8,128)(2,1)S(1)}, u32[]{:S(2)}, u32[]{:S(2)}) collective-permute-start(bf16[128,128]{0,1:T(8,128)(2,1)S(1)} %get-tuple-element.349), channel_id=1, source_target_pairs={{1,0},{2,1},{3,2},{4,3},{5,4},{6,5},{7,6},{9,8},{10,9},{11,10},{12... | collective-permute-start | bytes 98312 | tf_op jit(solution)/shard_map/ppermute | solution.py:14
  125.9 4.1 %collective-permute-done.7 = bf16[128,128]{0,1:T(8,128)(2,1)S(1)} collective-permute-done((bf16[128,128]{0,1:T(8,128)(2,1)S(1)}, bf16[128,128]{0,1:T(8,128)(2,1)S(1)}, u32[]{:S(2)}, u32[]{:S(2)}) %collective-permute-start.7) | collective-permute-done | bytes 32800 | tf_op jit(solution)/shard_map/ppermute | solution.py:14
  130.3 48.8 %while.38 = (s32[]{:T(128)}, f32[1024,128]{1,0:T(8,128)S(1)}, bf16[8,512,128]{2,1,0:T(8,128)(2,1)}, s32[8,512]{1,0:T(8,128)S(1)}, bf16[8,512,128]{1,2,0:T(8,128)...) while((s32[]{:T(128)}, f32[1024,128]{1,0:T(8,128)S(1)}, ...), condition=%wide.region_14.15_spmd.clone, body=%wide.region_11.14_spmd.clone.sunk | while | flops 541786624 | bytes 4495003 | solution.py:73
  131.6 1.5 fusion.186
  133.1 1.5 fusion.187
  137.7 1.5 fusion.186
  139.2 1.5 fusion.187
  143.8 1.5 fusion.186
  145.3 1.5 fusion.187
  149.9 1.5 fusion.186
  151.4 1.5 fusion.187
  156.0 1.5 fusion.186
  157.5 1.5 fusion.187
  162.1 1.5 fusion.186
  163.6 1.5 fusion.187
  168.2 1.5 fusion.186
  169.7 1.5 fusion.187
  174.3 1.5 fusion.186
  175.8 1.5 fusion.187
  (266 shorter events, 62.1 us)
Async XLA Ops:
  0.6 13.7 %copy-start = (bf16[1024,128]{1,0:T(8,128)(2,1)S(1)}, bf16[1024,128]{1,0:T(8,128)(2,1)}, u32[]{:S(2)}) copy-start(bf16[1024,128]{1,0:T(8,128)(2,1)} %param.22) | copy-start | bytes 786436
  0.6 13.9 %copy-start.1 = (bf16[2,384,128]{2,1,0:T(8,128)(2,1)S(1)}, bf16[2,384,128]{2,1,0:T(8,128)(2,1)}, u32[]{:S(2)}) copy-start(bf16[2,384,128]{2,1,0:T(8,128)(2,1)} %param.29) | copy-start | bytes 589828
  0.7 13.9 %copy-start.2 = (bf16[2,128,128]{2,1,0:T(8,128)(2,1)S(1)}, bf16[2,128,128]{2,1,0:T(8,128)(2,1)}, u32[]{:S(2)}) copy-start(bf16[2,128,128]{2,1,0:T(8,128)(2,1)} %param.30) | copy-start | bytes 196612
  0.7 14.5 %copy-start.7 = (f32[2,3,128]{2,0,1:T(2,128)S(1)}, f32[2,3,128]{2,0,1:T(2,128)}, u32[]{:S(2)}) copy-start(f32[2,3,128]{2,0,1:T(2,128)} %param.31) | copy-start | bytes 9220
  0.7 14.5 %copy-start.12 = (f32[2,128]{1,0:T(2,128)S(1)}, f32[2,128]{1,0:T(2,128)}, u32[]{:S(2)}) copy-start(f32[2,128]{1,0:T(2,128)} %param.32) | copy-start | bytes 3076
  2.2 33.4 %copy-start.11 = (f32[2,3,128]{2,0,1:T(2,128)S(1)}, f32[2,3,128]{2,0,1:T(2,128)}, u32[]{:S(2)}) copy-start(f32[2,3,128]{2,0,1:T(2,128)} %param.36) | copy-start | bytes 9220
  2.2 34.0 %copy-start.10 = (bf16[8,128]{1,0:T(8,128)(2,1)S(1)}, bf16[8,128]{1,0:T(8,128)(2,1)}, u32[]{:S(2)}) copy-start(bf16[8,128]{1,0:T(8,128)(2,1)} %param.27) | copy-start | bytes 6148
  2.2 55.9 %copy-start.6 = (s32[1024]{0:T(1024)S(1)}, s32[1024]{0:T(1024)}, u32[]{:S(2)}) copy-start(s32[1024]{0:T(1024)} %param.28) | copy-start | bytes 12292
  2.9 56.9 %collective-permute-start = (bf16[128,128]{1,0:T(8,128)(2,1)}, bf16[128,128]{1,0:T(8,128)(2,1)S(1)}, u32[]{:S(2)}, u32[]{:S(2)}) collective-permute-start(bf16[128,128]{1,0:T(8,128)(2,1)} %get-tuple-element.356), channel_id=1, source_target_pairs={{0,8},{8,16},{16,24},{1,9},{9,17},{17,25},{2,10},{10,18},{18,26},{... | collective-permute-start | bytes 98312 | tf_op jit(solution)/shard_map/ppermute | solution.py:14
  6.1 53.7 %collective-permute-start.1 = (bf16[128,128]{1,0:T(8,128)(2,1)}, bf16[128,128]{1,0:T(8,128)(2,1)S(1)}, u32[]{:S(2)}, u32[]{:S(2)}) collective-permute-start(bf16[128,128]{1,0:T(8,128)(2,1)} %get-tuple-element.355), channel_id=1, source_target_pairs={{8,0},{16,8},{24,16},{9,1},{17,9},{25,17},{10,2},{18,10},{26,18},{... | collective-permute-start | bytes 98312 | tf_op jit(solution)/shard_map/ppermute | solution.py:14
  8.2 51.6 %collective-permute-start.2 = (bf16[128,128]{1,0:T(8,128)(2,1)S(1)}, bf16[128,128]{1,0:T(8,128)(2,1)S(1)}, u32[]{:S(2)}, u32[]{:S(2)}) collective-permute-start(bf16[128,128]{1,0:T(8,128)(2,1)S(1)} %get-tuple-element.354), channel_id=1, source_target_pairs={{0,1},{1,2},{2,3},{3,4},{4,5},{5,6},{6,7},{8,9},{9,10},{10,11},{11... | collective-permute-start | bytes 98312 | tf_op jit(solution)/shard_map/ppermute | solution.py:14
  12.4 47.4 %collective-permute-start.3 = (bf16[128,128]{1,0:T(8,128)(2,1)S(1)}, bf16[128,128]{1,0:T(8,128)(2,1)S(1)}, u32[]{:S(2)}, u32[]{:S(2)}) collective-permute-start(bf16[128,128]{1,0:T(8,128)(2,1)S(1)} %get-tuple-element.353), channel_id=1, source_target_pairs={{1,0},{2,1},{3,2},{4,3},{5,4},{6,5},{7,6},{9,8},{10,9},{11,10},{12... | collective-permute-start | bytes 98312 | tf_op jit(solution)/shard_map/ppermute | solution.py:14
  15.2 43.6 %copy-start.13 = (f32[2,128]{1,0:T(2,128)S(1)}, f32[2,128]{1,0:T(2,128)}, u32[]{:S(2)}) copy-start(f32[2,128]{1,0:T(2,128)} %param.37) | copy-start | bytes 3076
  15.2 44.1 %copy-start.16 = (bf16[2,128,128]{2,1,0:T(8,128)(2,1)S(1)}, bf16[2,128,128]{2,1,0:T(8,128)(2,1)}, u32[]{:S(2)}) copy-start(bf16[2,128,128]{2,1,0:T(8,128)(2,1)} %param.34) | copy-start | bytes 196612
  58.1 1.4 copy-start.4
  58.1 1.4 copy-start.5
  110.7 1.7 copy-start.8
  110.7 1.7 copy-start.9
  112.2 0.7 copy-start.18
  112.3 5.2 %copy-start.17 = (bf16[2,128,128]{2,1,0:T(8,128)(2,1)S(1)}, bf16[2,128,128]{2,1,0:T(8,128)(2,1)}, u32[]{:S(2)}) copy-start(bf16[2,128,128]{2,1,0:T(8,128)(2,1)} %param.34) | copy-start | bytes 196612
  113.5 16.7 %copy-start.3 = (bf16[128,128]{1,0:T(8,128)(2,1)S(1)}, bf16[128,128]{1,0:T(8,128)(2,1)}, u32[]{:S(2)}) copy-start(bf16[128,128]{1,0:T(8,128)(2,1)} %get-tuple-element.643) | copy-start | bytes 98308
  113.6 12.2 %collective-permute-start.4 = (bf16[128,128]{0,1:T(8,128)(2,1)S(1)}, bf16[128,128]{0,1:T(8,128)(2,1)S(1)}, u32[]{:S(2)}, u32[]{:S(2)}) collective-permute-start(bf16[128,128]{0,1:T(8,128)(2,1)S(1)} %get-tuple-element.352), channel_id=1, source_target_pairs={{0,8},{8,16},{16,24},{1,9},{9,17},{17,25},{2,10},{10,18},{18,26},{... | collective-permute-start | bytes 98312 | tf_op jit(solution)/shard_map/ppermute | solution.py:14
  118.5 7.3 %collective-permute-start.5 = (bf16[128,128]{0,1:T(8,128)(2,1)S(1)}, bf16[128,128]{0,1:T(8,128)(2,1)S(1)}, u32[]{:S(2)}, u32[]{:S(2)}) collective-permute-start(bf16[128,128]{0,1:T(8,128)(2,1)S(1)} %get-tuple-element.351), channel_id=1, source_target_pairs={{8,0},{16,8},{24,16},{9,1},{17,9},{25,17},{10,2},{18,10},{26,18},{... | collective-permute-start | bytes 98312 | tf_op jit(solution)/shard_map/ppermute | solution.py:14
  120.5 5.4 %collective-permute-start.6 = (bf16[128,128]{0,1:T(8,128)(2,1)S(1)}, bf16[128,128]{0,1:T(8,128)(2,1)S(1)}, u32[]{:S(2)}, u32[]{:S(2)}) collective-permute-start(bf16[128,128]{0,1:T(8,128)(2,1)S(1)} %get-tuple-element.350), channel_id=1, source_target_pairs={{0,1},{1,2},{2,3},{3,4},{4,5},{5,6},{6,7},{8,9},{9,10},{10,11},{11... | collective-permute-start | bytes 98312 | tf_op jit(solution)/shard_map/ppermute | solution.py:14
  123.9 6.1 %collective-permute-start.7 = (bf16[128,128]{0,1:T(8,128)(2,1)S(1)}, bf16[128,128]{0,1:T(8,128)(2,1)S(1)}, u32[]{:S(2)}, u32[]{:S(2)}) collective-permute-start(bf16[128,128]{0,1:T(8,128)(2,1)S(1)} %get-tuple-element.349), channel_id=1, source_target_pairs={{1,0},{2,1},{3,2},{4,3},{5,4},{6,5},{7,6},{9,8},{10,9},{11,10},{12... | collective-permute-start | bytes 98312 | tf_op jit(solution)/shard_map/ppermute | solution.py:14
  130.2 49.0 %copy-start.14 = (f32[128]{0:T(128)S(1)}, f32[128]{0:T(128)}, u32[]{:S(2)}) copy-start(f32[128]{0:T(128)} %get-tuple-element.362) | copy-start | bytes 1540
  130.3 49.0 %copy-start.15 = (bf16[2,384,128]{2,1,0:T(8,128)(2,1)S(1)}, bf16[2,384,128]{2,1,0:T(8,128)(2,1)}, u32[]{:S(2)}) copy-start(bf16[2,384,128]{2,1,0:T(8,128)(2,1)} %param.33) | copy-start | bytes 589828
